TPU v7x, 32 devices: a whole 2x2x4 slice. The times are simulated.
32 devices in a mesh: dp: 16 (over z, x, core), mp: 2 (over y).
Axes of the slice: x: 2, y: 2, z: 4, core: 2. Of those that a mesh axis runs over, the one named last changes fastest.
Arguments:
- tokens: bfloat16 [192, 4608], P('dp', 'mp'), may hold values from -6 to 6
- frozen_weight: bfloat16 [2, 4608, 36864], P(None, 'mp', 'dp'), may hold values from -36 to 36
- adapter_down: bfloat16 [2, 16, 4608], P(None, None, 'mp'), may hold values from -1.5 to 1.5
- adapter_up: bfloat16 [2, 16, 36864], P(None, None, 'dp'), may hold values from -3 to 3
- magnitude: float32 [2, 36864], P(None, 'dp'), may hold values from 0.5 to 2
- hidden_gradient: bfloat16 [192, 36864], P('mp', 'dp'), may hold values from -0.59765625 to 0.59765625
Outputs:
- hidden: bfloat16 [192, 36864], P('mp', 'dp')
- token_gradient: float32 [192, 4608], P('dp', 'mp')
- adapter_down_gradient: float32 [2, 16, 4608], P(None, None, 'mp')
- adapter_up_gradient: float32 [2, 16, 36864], P(None, None, 'dp')
- magnitude_gradient: float32 [2, 36864], P(None, 'dp')
All inputs are finite; a program needn't handle non-finite values.
Results may differ from a plain program's by a relative error of at most 0.023.
Values may be sent and summed in bfloat16 or wider, within the bound.
A program may use at most 64 MiB of HBM per device.

v0:
```python
import jax
import jax.numpy as jnp
from jax import lax
from jax.sharding import PartitionSpec as P

LOWRANK_SCALE = 2.0
EPSILON = 1e-06
MATMUL_ACCURACY = lax.Precision.HIGHEST


def gelu_pair(source):
    cubic_term = source + 0.044715 * source * source * source
    tangent = jnp.tanh(0.7978845608028654 * cubic_term)
    result = 0.5 * source * (1.0 + tangent)
    derivative = 0.5 * (1.0 + tangent) + 0.5 * source * (
        1.0 - tangent * tangent
    ) * 0.7978845608028654 * (1.0 + 0.134145 * source * source)
    return (result, derivative)


def on_device(tokens, frozen_weight, adapter_down, adapter_up, magnitude, hidden_gradient):
    every_row = lax.all_gather(tokens, "dp", axis=0, tiled=True)
    down_broad = adapter_down.astype(jnp.float32)
    up_broad = adapter_up.astype(jnp.float32)
    base_square = jnp.sum(jnp.square(frozen_weight.astype(jnp.float32)), axis=1)
    cross_base = jnp.einsum(
        "krd,kdf->krf", adapter_down, frozen_weight, preferred_element_type=jnp.float32
    )
    gram_part = jnp.einsum(
        "krd,ksd->krs", adapter_down, adapter_down, preferred_element_type=jnp.float32
    )
    square_base, cross_total, gram_sum = (
        lax.psum(base_square.astype(jnp.bfloat16), "mp").astype(jnp.float32),
        lax.psum(cross_base.astype(jnp.bfloat16), "mp").astype(jnp.float32),
        lax.psum(gram_part.astype(jnp.bfloat16), "mp").astype(jnp.float32),
    )
    gram_up = jnp.einsum("krs,ksf->krf", gram_sum, up_broad, precision=MATMUL_ACCURACY)
    mixed_sum = cross_total + LOWRANK_SCALE * gram_up
    square_sum = (
        square_base
        + 2.0 * LOWRANK_SCALE * jnp.sum(up_broad * cross_total, axis=1)
        + LOWRANK_SCALE * LOWRANK_SCALE * jnp.sum(up_broad * gram_up, axis=1)
    )
    base_part = jnp.einsum(
        "td,kdf->ktf", every_row, frozen_weight, preferred_element_type=jnp.float32
    )
    lowrank_piece = jnp.einsum(
        "su,vgu->vsg", every_row, adapter_down, preferred_element_type=jnp.float32
    )
    col_norm = jnp.sqrt(square_sum + EPSILON)
    col_ratio = magnitude / col_norm
    share_rows = every_row.shape[0] // lax.axis_size("mp")
    base_sum, low_sum = (
        lax.psum(base_part.astype(jnp.bfloat16), "mp").astype(jnp.float32),
        lax.psum(lowrank_piece.astype(jnp.bfloat16), "mp").astype(jnp.float32),
    )
    cot_rows = lax.all_gather(hidden_gradient, "mp", axis=0, tiled=True)
    token_lowrank = low_sum.astype(jnp.bfloat16)
    unscaled_output = base_sum + LOWRANK_SCALE * jnp.einsum(
        "hls,hse->hle", token_lowrank, adapter_up, preferred_element_type=jnp.float32
    )
    gate_proj = unscaled_output[0] * col_ratio[0]
    up_proj = unscaled_output[1] * col_ratio[1]
    activated, derivative = gelu_pair(gate_proj)
    hidden_rows = (activated * up_proj).astype(jnp.bfloat16)
    cotangent = cot_rows.astype(jnp.float32)
    grad_out = jnp.stack([cotangent * up_proj * derivative, cotangent * activated])
    moment_part = jnp.sum(grad_out * unscaled_output, axis=1)
    prescale_gradient = (grad_out * col_ratio[:, None, :]).astype(jnp.bfloat16)
    lowrank_gradient_piece = jnp.einsum(
        "hmu,hmq->huq", token_lowrank, prescale_gradient, preferred_element_type=jnp.float32
    )
    hidden = lax.dynamic_slice_in_dim(hidden_rows, lax.axis_index("mp") * share_rows, share_rows, 0)
    magnitude_gradient = moment_part / col_norm
    frozen_term = -magnitude * moment_part / (col_norm * col_norm * col_norm)
    adapter_up_gradient = LOWRANK_SCALE * (
        lowrank_gradient_piece + mixed_sum * frozen_term[:, None, :]
    )
    lowrank_gradient = jnp.einsum(
        "pge,pbe->pgb", prescale_gradient, adapter_up, preferred_element_type=jnp.float32
    ).astype(jnp.bfloat16)
    weighted_adapter_up = up_broad * frozen_term[:, None, :]
    broadcast_value = jnp.einsum(
        "krf,kdf->krd",
        weighted_adapter_up,
        frozen_weight.astype(jnp.float32),
        precision=MATMUL_ACCURACY,
    )
    inner_gram = jnp.einsum(
        "krf,ksf->krs", weighted_adapter_up, up_broad, precision=MATMUL_ACCURACY
    )
    broadcast_value = broadcast_value + LOWRANK_SCALE * jnp.einsum(
        "krs,ksd->krd", inner_gram, down_broad, precision=MATMUL_ACCURACY
    )
    down_piece = LOWRANK_SCALE * (
        jnp.einsum("ijp,jv->ipv", lowrank_gradient, every_row, preferred_element_type=jnp.float32)
        + broadcast_value
    )
    adapter_down_gradient = lax.psum(down_piece, "dp")
    main_term = jnp.einsum(
        "ktf,kdf->td", prescale_gradient, frozen_weight, preferred_element_type=jnp.float32
    )
    token_gradient = lax.psum_scatter(
        main_term
        + LOWRANK_SCALE
        * jnp.einsum(
            "ijf,ifh->jh", lowrank_gradient, adapter_down, preferred_element_type=jnp.float32
        ),
        "dp",
        scatter_dimension=0,
        tiled=True,
    )
    return (hidden, token_gradient, adapter_down_gradient, adapter_up_gradient, magnitude_gradient)


def solution(mesh):
    in_specs = (
        P("dp", "mp"),
        P(None, "mp", "dp"),
        P(None, None, "mp"),
        P(None, None, "dp"),
        P(None, "dp"),
        P("mp", "dp"),
    )
    out_specs = (
        P("mp", "dp"),
        P("dp", "mp"),
        P(None, None, "mp"),
        P(None, None, "dp"),
        P(None, "dp"),
    )
    return jax.shard_map(
        on_device, mesh=mesh, in_specs=in_specs, out_specs=out_specs, check_vma=False
    )
```

profile of v0, /device:TPU:0, one launch (start us, length us, event | category | flops | bytes accessed | tf_op | source)
XLA Modules:
  0.0 308.0 jit_solution(16763437248531426310)
XLA Ops:
  7.2 26.6 %all-gather = bf16[16,12,2304]{2,1,0:T(8,128)(2,1)S(1)} all-gather(bf16[1,12,2304]{2,1,0:T(8,128)(2,1)} %bitcast.66), channel_id=1, replica_groups=mesh['dp'=16,'mp'=2] {'dp'}, dimensions={0}, use_global_device_ids=true | all-gather | bytes 940032 | tf_op jit(solution)/shard_map/all_gather | solution.py:22
  34.1 12.7 %fusion.2 = bf16[2,192,2304]{2,1,0:T(8,128)(2,1)} fusion(bf16[192,2304,1]{1,0,2:T(8,128)(2,1)S(1)} %reshape.14, bf16[2,2304,2304]{2,1,0:T(8,128)(2,1)} %param.7), kind=kOutput, calls=%fused_computation.4 | convolution fusion | flops 4077748224 | bytes 23887872 | tf_op jit(solution)/shard_map/td,kdf->ktf/dot_general | solution.py:44
  46.8 1.0 copy-done.1
  47.8 3.5 %convolution_convert_fusion.1 = bf16[2,16,2304]{2,1,0:T(8,128)(2,1)} fusion(bf16[2,16,2304]{2,1,0:T(8,128)(2,1)S(1)} %copy-done, bf16[2,2304,2304]{2,1,0:T(8,128)(2,1)S(1)} %copy-done.1), kind=kOutput, calls=%fused_computation.18 | convolution fusion | flops 339812352 | bytes 21528576 | tf_op jit(solution)/shard_map/krd,kdf->krf/dot_general | solution.py:26
  51.6 0.4 copy-done.8
  52.0 0.6 dynamic-slice.4
  53.6 9.3 %multiply_reduce_fusion = bf16[2,2304]{1,0:T(2,128)(2,1)S(1)} fusion(bf16[2,2304,2304]{2,1,0:T(8,128)(2,1)} %param.7), kind=kLoop, calls=%fused_computation | loop fusion | flops 31845888 | bytes 21242880 | tf_op jit(solution)/shard_map/reduce_sum | solution.py:25
  62.9 9.7 %all-reduce.2 = (bf16[2,192,16]{1,2,0:T(8,128)(2,1)S(1)}, bf16[2,16,16]{2,1,0:T(8,128)(2,1)S(1)}, bf16[2,2304]{1,0:T(2,128)(2,1)S(1)}) all-reduce(bf16[2,192,16]{1,2,0:T(8,128)(2,1)S(1)} %fusion.18, bf16[2,16,16]{2,1,0:T(8,128)(2,1)S(1)} %convolution_convert_fusion.4, ...), channel_id=1, replica_groups=mesh['dp'=16,'mp'=2] {'mp'}, use_global_device_ids=true, to_apply=%region_1.0 | all-reduce | flops 11264 | bytes 45056 | tf_op jit(solution)/shard_map/psum | solution.py:55
  72.7 14.4 %all_gather.7 = bf16[192,2304]{1,0:T(8,128)(2,1)S(1)} all-gather(bf16[96,2304]{1,0:T(8,128)(2,1)S(1)} %copy-done.4), channel_id=1, replica_groups=mesh['dp'=16,'mp'=2] {'mp'}, dimensions={0}, use_global_device_ids=true | all-gather | bytes 1327104 | tf_op jit(solution)/shard_map/all_gather | solution.py:57
  87.1 29.1 %all-reduce.9.cloned.1.call-done = (bf16[2,192,2304]{2,1,0:T(8,128)(2,1)}, bf16[2,16,2304]{2,1,0:T(8,128)(2,1)}) async-done(((bf16[2,192,2304]{2,1,0:T(8,128)(2,1)}, bf16[2,16,2304]{2,1,0:T(8,128)(2,1)}), (bf16[2,192,2304]{2,1,0:T(8,128)(2,1)}, bf16[2,16,2304]{2,1,0:T(8,128)(2,1)})) %all-reduce.9.cloned.1.call-update) | async-done | bytes 1916944 | tf_op jit(solution)/shard_map/psum | solution.py:54
  116.1 1.1 fusion.22
  117.3 0.7 fusion.28
  118.0 2.1 fusion.1
  120.1 3.2 %fusion.10 = (f32[1,192,2304]{2,1,0:T(8,128)S(1)}, f32[192,2304]{1,0:T(8,128)}, f32[1,192,2304]{2,1,0:T(8,128)S(1)}, f32[192,2304]{1,0:T(8,128)}) fusion(bf16[192,2304]{1,0:T(8,128)(2,1)S(1)} %all_gather.7, f32[2304]{0:T(1024)S(1)} %get-tuple-element.7, f32[2,192,2304]{2,1,0:T(8,128)S(1)} %fusion.1, f32[2304]{0:T(1024)S(1)} %get-tuple-element.8), kind=kLoop, calls=%fused_computation.25 | loop fusion | flops 10616832 | bytes 11520000 | tf_op jit(solution)/shard_map/stack | solution.py:67
  123.3 1.1 multiply_reduce_fusion.1
  124.4 11.2 %convolution_bitcast_fusion = f32[192,2304]{1,0:T(8,128)S(1)} fusion(bf16[2,192,2304]{2,1,0:T(8,128)(2,1)S(1)} %get-tuple-element.23, bf16[2,2304,2304]{2,1,0:T(8,128)(2,1)} %param.7), kind=kOutput, calls=%fused_computation.5 | convolution fusion | flops 4076863488 | bytes 24772608 | tf_op jit(solution)/shard_map/ktf,kdf->td/dot_general | solution.py:100
  135.7 0.6 convolution_convert_fusion.2
  136.2 1.7 fusion.4
  137.9 41.5 %fusion = f32[16,2304]{1,0:T(8,128)S(1)} fusion(f32[192,2304]{1,0:T(8,128)} %fusion.4), kind=kCustom, calls=%all-reduce-scatter | all-reduce-scatter fusion | flops 589825 | bytes 1917440
  179.3 0.7 slice.20
  180.0 1.3 collective-permute-start.2
  181.3 2.0 collective-permute-start.1
  183.3 1.9 collective-permute-start
  185.5 1.3 collective-permute-start.3
  186.8 1.4 fusion.29
  188.8 20.5 %fusion.7 = f32[2,16,2304]{2,1,0:T(8,128)} fusion(f32[2,16,2304]{2,1,0:T(8,128)S(1)} %fusion.30, f32[2,16,2304]{2,1,0:T(8,128)S(1)} %convolution_multiply_fusion.1, bf16[2,2304,2304]{2,1,0:T(8,128)(2,1)} %param.7, bf16[2,16,2304]{2,1,0:T(8,128)(2,1)S(1)} %copy-done.2, f32[2,2304]{1,0:T(2,128)S(1)} %get-tuple-element.25), kind=kOutput, calls=%fused_computation.17 | convolution fusion | flops 2038800384 | bytes 22284288 | tf_op jit(solution)/shard_map/krf,kdf->krd/dot_general | solution.py:83
  209.4 2.3 fusion.19
  211.7 1.1 fusion.5
  212.8 2.5 concatenate
  215.3 0.7 constant_dynamic-slice_fusion
  215.9 83.6 %all-reduce.7.cloned.1.call-done = f32[2,16,2304]{2,1,0:T(8,128)} async-done(((f32[2,16,2304]{2,1,0:T(8,128)}), f32[2,16,2304]{2,1,0:T(8,128)}) %all-reduce.7.cloned.1.call-update) | async-done | bytes 294928 | tf_op jit(solution)/shard_map/psum | solution.py:99
  299.5 1.7 copy.14
  (31 shorter events, 1.8 us)
Async XLA Ops:
  7.2 39.6 %copy-start = (bf16[2,16,2304]{2,1,0:T(8,128)(2,1)S(1)}, bf16[2,16,2304]{2,1,0:T(8,128)(2,1)}, u32[]{:S(2)}) copy-start(bf16[2,16,2304]{2,1,0:T(8,128)(2,1)} %param.8) | copy-start | bytes 442372
  7.2 108.9 %all-reduce.9.cloned.1.call-start = ((), (), s32[]{:S(2)}) async-start(), calls=%async_computation.1 | async-start | bytes 3833856 | tf_op jit(solution)/shard_map/psum | solution.py:54
  34.1 13.7 %copy-start.1 = (bf16[2,2304,2304]{2,1,0:T(8,128)(2,1)S(1)}, bf16[2,2304,2304]{2,1,0:T(8,128)(2,1)}, u32[]{:S(2)}) copy-start(bf16[2,2304,2304]{2,1,0:T(8,128)(2,1)} %param.7) | copy-start | bytes 63700996
  51.3 0.7 copy-start.8
  51.3 248.1 %all-reduce.7.cloned.1.call-start = ((), (), s32[]{:S(2)}) async-start(), calls=%async_computation | async-start | bytes 589824 | tf_op jit(solution)/shard_map/psum | solution.py:99
  53.6 19.1 %copy-start.4 = (bf16[96,2304]{1,0:T(8,128)(2,1)S(1)}, bf16[96,2304]{1,0:T(8,128)(2,1)}, u32[]{:S(2)}) copy-start(bf16[96,2304]{1,0:T(8,128)(2,1)} %param.11) | copy-start | bytes 1327108
  53.6 62.5 %copy-start.2 = (bf16[2,16,2304]{2,1,0:T(8,128)(2,1)S(1)}, bf16[2,16,2304]{2,1,0:T(8,128)(2,1)}, u32[]{:S(2)}) copy-start(bf16[2,16,2304]{2,1,0:T(8,128)(2,1)} %param.9) | copy-start | bytes 442372
  62.9 54.4 %copy-start.5 = (f32[2,2304]{1,0:T(2,128)S(1)}, f32[2,2304]{1,0:T(2,128)}, u32[]{:S(2)}) copy-start(f32[2,2304]{1,0:T(2,128)} %param.10) | copy-start | bytes 55300
  72.7 47.4 %copy-start.6 = (bf16[2,192,16]{1,2,0:T(8,128)(2,1)}, bf16[2,192,16]{1,2,0:T(8,128)(2,1)S(1)}, u32[]{:S(2)}) copy-start(bf16[2,192,16]{1,2,0:T(8,128)(2,1)S(1)} %get-tuple-element.9) | copy-start | bytes 36868
  180.0 32.7 %collective-permute-start.2 = (f32[16,2304]{1,0:T(8,128)S(1)}, f32[16,2304]{1,0:T(8,128)S(1)}, u32[]{:S(2)}, u32[]{:S(2)}) collective-permute-start(f32[16,2304]{1,0:T(8,128)S(1)} %fusion), channel_id=1, source_target_pairs={{0,6},{2,8},{4,10},{6,12},{8,14},{10,16},{12,18},{14,20},{16,22},{... | collective-permute-start | bytes 442376
  181.3 31.4 %collective-permute-start.1 = (f32[16,2304]{1,0:T(8,128)S(1)}, f32[16,2304]{1,0:T(8,128)}, u32[]{:S(2)}, u32[]{:S(2)}) collective-permute-start(f32[16,2304]{1,0:T(8,128)S(1)} %fusion), channel_id=1, source_target_pairs={{0,4},{2,6},{4,8},{6,10},{8,12},{10,14},{12,16},{14,18},{16,20},{1... | collective-permute-start | bytes 442376
  183.3 29.5 %collective-permute-start = (f32[16,2304]{1,0:T(8,128)S(1)}, f32[16,2304]{1,0:T(8,128)}, u32[]{:S(2)}, u32[]{:S(2)}) collective-permute-start(f32[16,2304]{1,0:T(8,128)S(1)} %fusion), channel_id=1, source_target_pairs={{0,2},{2,4},{4,6},{6,8},{8,10},{10,12},{12,14},{14,16},{16,18},{18... | collective-permute-start | bytes 442376
  185.5 27.2 %collective-permute-start.3 = (f32[12,2304]{1,0:T(8,128)}, f32[12,2304]{1,0:T(8,128)S(1)}, u32[]{:S(2)}, u32[]{:S(2)}) collective-permute-start(f32[12,2304]{1,0:T(8,128)} %slice.20), channel_id=1, source_target_pairs={{0,8},{2,10},{4,12},{6,14},{8,16},{10,18},{12,20},{14,22},{16,24},... | collective-permute-start | bytes 331784
  209.3 2.4 copy-start.3
  209.3 2.4 copy-start.7
Sparse Core Ops, SparseCore 0:
  51.5 64.5 all-reduce.8
  209.5 89.9 all-reduce.6
where the time goes:
time: 309 us; the launch traced here: 308 us
  waiting for transfers between devices  113 us (37%)
  blocking collectives  92.2 us (30%)
  matrix products  55.8 us (18%)
  other arithmetic  18 us (6%)
  between operations  14.9 us (5%)
  local copies, waits for them, and re-layouts  7.86 us (3%)
  starting transfers between devices  6.56 us (2%)
    psum x1, waiting for transfers between devices, on_device(): adapter_down_gradient = lax.psum(down_piece, 'dp')  83.6 us
    unnamed x1, blocking collectives  41.5 us
    psum x1, waiting for transfers between devices, on_device(): lax.psum(base_part.astype(jnp.bfloat16), 'mp').astype(jnp.float32)  29.1 us
    all_gather x1, blocking collectives, on_device(): every_row = lax.all_gather(tokens, 'dp', axis=0, tiled=True)  26.6 us
    dot_general x1, matrix products, on_device(): jnp.einsum('krf,kdf->krd', weighted_adapter_up, frozen_weight.astype(jnp....  20.5 us
    all_gather x1, blocking collectives, on_device(): cot_rows = lax.all_gather(hidden_gradient, 'mp', axis=0, tiled=True)  14.4 us
    dot_general x1, matrix products, on_device(): jnp.einsum('td,kdf->ktf', every_row, frozen_weight, preferred_element_typ...  12.7 us
    dot_general x1, matrix products, on_device(): jnp.einsum('ktf,kdf->td', prescale_gradient, frozen_weight, preferred_ele...  11.2 us
  transfers between devices with their start and end apart: 6, of which 2 were waited for; matrix products, arithmetic and copies ran while one was open for 13% of the time, Pallas kernels for 0%

commit v1 on v0

--- a/solution.py
+++ b/solution.py
@@ -96,7 +96,7 @@
         jnp.einsum("ijp,jv->ipv", lowrank_gradient, every_row, preferred_element_type=jnp.float32)
         + broadcast_value
     )
-    adapter_down_gradient = lax.psum(down_piece, "dp")
+    adapter_down_gradient = jax.lax.all_gather(down_piece, "dp").sum(axis=0)
     main_term = jnp.einsum(
         "ktf,kdf->td", prescale_gradient, frozen_weight, preferred_element_type=jnp.float32
     )

time: 309 us -> 235 us (0.76)
  waiting for transfers between devices: 113 us -> 30.5 us
  blocking collectives: 92.2 us -> 99.1 us
  starting transfers between devices: 6.56 us -> 11.2 us
  local copies, waits for them, and re-layouts: 7.86 us -> 3.36 us
    psum x1 -> x0, waiting for transfers between devices: 83.6 us -> none  [on_device(): adapter_down_gradient = lax.psum(down_piece, 'dp')]
    unnamed x1, blocking collectives: 41.5 us -> 46.9 us
    unnamed x4, starting transfers between devices: 6.48 us -> 11.1 us
    unnamed x24 -> x19, local copies, waits for them, and re-layouts: 7.81 us -> 3.31 us
    reduce_sum x0 -> x1, other arithmetic: none -> 3.29 us  [on_device(): adapter_down_gradient = jax.lax.all_gather(down_piece, 'dp').sum(axis=0)]
  transfers between devices with their start and end apart: 6 -> 6, of which waited for: 2 -> 1; matrix products, arithmetic and copies ran while one was open for 13% -> 32% of each run, Pallas kernels for 0% -> 0%
where the time goes in v1:
time: 235 us; the launch traced here: 234 us
  blocking collectives  99.1 us (42%)
  matrix products  56 us (24%)
  waiting for transfers between devices  30.5 us (13%)
  other arithmetic  19.4 us (8%)
  between operations  14.9 us (6%)
  starting transfers between devices  11.2 us (5%)
  local copies, waits for them, and re-layouts  3.36 us (1%)
    unnamed x1, blocking collectives  46.9 us
    psum x1, waiting for transfers between devices, on_device(): lax.psum(base_part.astype(jnp.bfloat16), 'mp').astype(jnp.float32)  30.5 us
    all_gather x1, blocking collectives, on_device(): every_row = lax.all_gather(tokens, 'dp', axis=0, tiled=True)  26.6 us
    dot_general x1, matrix products, on_device(): jnp.einsum('krf,kdf->krd', weighted_adapter_up, frozen_weight.astype(jnp....  20.5 us
    all_gather x1, blocking collectives, on_device(): cot_rows = lax.all_gather(hidden_gradient, 'mp', axis=0, tiled=True)  16.1 us
    dot_general x1, matrix products, on_device(): jnp.einsum('td,kdf->ktf', every_row, frozen_weight, preferred_element_typ...  12.7 us
    dot_general x1, matrix products, on_device(): jnp.einsum('ktf,kdf->td', prescale_gradient, frozen_weight, preferred_ele...  11.2 us
    unnamed x4, starting transfers between devices  11.1 us
  transfers between devices with their start and end apart: 6, of which 1 were waited for; matrix products, arithmetic and copies ran while one was open for 32% of the time, Pallas kernels for 0%

profile of v1, /device:TPU:0, one launch (start us, length us, event | category | flops | bytes accessed | tf_op | source)
XLA Modules:
  0.0 234.5 jit_solution(13715816120449273330)
XLA Ops:
  7.2 26.6 %all-gather.1 = bf16[16,12,2304]{2,1,0:T(8,128)(2,1)S(1)} all-gather(bf16[1,12,2304]{2,1,0:T(8,128)(2,1)} %bitcast.68), channel_id=1, replica_groups=mesh['dp'=16,'mp'=2] {'dp'}, dimensions={0}, use_global_device_ids=true | all-gather | bytes 940032 | tf_op jit(solution)/shard_map/all_gather | solution.py:22
  34.1 12.7 %fusion.2 = bf16[2,192,2304]{2,1,0:T(8,128)(2,1)} fusion(bf16[192,2304,1]{1,0,2:T(8,128)(2,1)S(1)} %reshape.15, bf16[2,2304,2304]{2,1,0:T(8,128)(2,1)} %param.7), kind=kOutput, calls=%fused_computation.4 | convolution fusion | flops 4077748224 | bytes 23887872 | tf_op jit(solution)/shard_map/td,kdf->ktf/dot_general | solution.py:44
  46.8 1.0 copy-done.1
  47.8 3.5 %convolution_convert_fusion.1 = bf16[2,16,2304]{2,1,0:T(8,128)(2,1)} fusion(bf16[2,16,2304]{2,1,0:T(8,128)(2,1)S(1)} %copy-done, bf16[2,2304,2304]{2,1,0:T(8,128)(2,1)S(1)} %copy-done.1), kind=kOutput, calls=%fused_computation.18 | convolution fusion | flops 339812352 | bytes 21528576 | tf_op jit(solution)/shard_map/krd,kdf->krf/dot_general | solution.py:26
  51.5 0.4 fusion.18
  52.0 9.4 %multiply_reduce_fusion = bf16[2,2304]{1,0:T(2,128)(2,1)S(1)} fusion(bf16[2,2304,2304]{2,1,0:T(8,128)(2,1)} %param.7), kind=kLoop, calls=%fused_computation | loop fusion | flops 31845888 | bytes 21242880 | tf_op jit(solution)/shard_map/reduce_sum | solution.py:25
  61.4 9.5 %all-reduce.2 = (bf16[2,192,16]{1,2,0:T(8,128)(2,1)S(1)}, bf16[2,16,16]{2,1,0:T(8,128)(2,1)S(1)}, bf16[2,2304]{1,0:T(2,128)(2,1)S(1)}) all-reduce(bf16[2,192,16]{1,2,0:T(8,128)(2,1)S(1)} %fusion.18, bf16[2,16,16]{2,1,0:T(8,128)(2,1)S(1)} %convolution_convert_fusion.4, ...), channel_id=1, replica_groups=mesh['dp'=16,'mp'=2] {'mp'}, use_global_device_ids=true, to_apply=%region_1.0 | all-reduce | flops 11264 | bytes 45056 | tf_op jit(solution)/shard_map/psum | solution.py:55
  71.0 16.1 %all_gather.13 = bf16[192,2304]{1,0:T(8,128)(2,1)S(1)} all-gather(bf16[96,2304]{1,0:T(8,128)(2,1)S(1)} %copy-done.4), channel_id=1, replica_groups=mesh['dp'=16,'mp'=2] {'mp'}, dimensions={0}, use_global_device_ids=true | all-gather | bytes 1327104 | tf_op jit(solution)/shard_map/all_gather | solution.py:57
  87.1 30.5 %all-reduce.6.cloned.1.call-done = (bf16[2,192,2304]{2,1,0:T(8,128)(2,1)}, bf16[2,16,2304]{2,1,0:T(8,128)(2,1)}) async-done(((bf16[2,192,2304]{2,1,0:T(8,128)(2,1)}, bf16[2,16,2304]{2,1,0:T(8,128)(2,1)}), (bf16[2,192,2304]{2,1,0:T(8,128)(2,1)}, bf16[2,16,2304]{2,1,0:T(8,128)(2,1)})) %all-reduce.6.cloned.1.call-update) | async-done | bytes 1916944 | tf_op jit(solution)/shard_map/psum | solution.py:54
  117.5 1.1 fusion.22
  118.8 2.1 fusion.1
  120.9 3.2 %fusion.10 = (f32[1,192,2304]{2,1,0:T(8,128)S(1)}, f32[192,2304]{1,0:T(8,128)}, f32[1,192,2304]{2,1,0:T(8,128)S(1)}, f32[192,2304]{1,0:T(8,128)}) fusion(bf16[192,2304]{1,0:T(8,128)(2,1)S(1)} %all_gather.13, f32[2304]{0:T(1024)S(1)} %get-tuple-element.7, f32[2,192,2304]{2,1,0:T(8,128)S(1)} %fusion.1, f32[2304]{0:T(1024)S(1)} %get-tuple-element.8), kind=kLoop, calls=%fused_computation.25 | loop fusion | flops 10616832 | bytes 11520000 | tf_op jit(solution)/shard_map/stack | solution.py:67
  124.1 0.5 multiply_reduce_fusion.1
  124.6 0.6 convolution_convert_fusion.2
  125.2 0.3 fusion.30
  125.5 0.6 fusion.29
  126.1 0.3 fusion.20
  126.5 0.3 convolution_multiply_fusion.1
  126.8 20.5 %fusion.7 = f32[2,16,2304]{2,1,0:T(8,128)} fusion(f32[2,16,2304]{2,1,0:T(8,128)S(1)} %fusion.30, f32[2,16,2304]{2,1,0:T(8,128)S(1)} %convolution_multiply_fusion.1, bf16[2,2304,2304]{2,1,0:T(8,128)(2,1)} %param.7, bf16[2,16,2304]{2,1,0:T(8,128)(2,1)S(1)} %copy-done.2, f32[2,2304]{1,0:T(2,128)S(1)} %get-tuple-element.25), kind=kOutput, calls=%fused_computation.17 | convolution fusion | flops 2038800384 | bytes 22284288 | tf_op jit(solution)/shard_map/krf,kdf->krd/dot_general | solution.py:83
  147.3 0.6 dynamic-slice.4
  148.6 11.2 %convolution_bitcast_fusion = f32[192,2304]{1,0:T(8,128)S(1)} fusion(bf16[2,192,2304]{2,1,0:T(8,128)(2,1)S(1)} %get-tuple-element.23, bf16[2,2304,2304]{2,1,0:T(8,128)(2,1)} %param.7), kind=kOutput, calls=%fused_computation.5 | convolution fusion | flops 4076863488 | bytes 24772608 | tf_op jit(solution)/shard_map/ktf,kdf->td/dot_general | solution.py:100
  159.8 1.7 fusion.4
  161.5 46.9 %fusion = f32[16,2304]{1,0:T(8,128)S(1)} fusion(f32[192,2304]{1,0:T(8,128)} %fusion.4), kind=kCustom, calls=%all-reduce-scatter | all-reduce-scatter fusion | flops 589825 | bytes 1917440
  208.4 1.3 collective-permute-start.2
  209.7 2.7 %collective-permute-start.1 = (f32[16,2304]{1,0:T(8,128)S(1)}, f32[16,2304]{1,0:T(8,128)S(1)}, u32[]{:S(2)}, u32[]{:S(2)}) collective-permute-start(f32[16,2304]{1,0:T(8,128)S(1)} %fusion), channel_id=1, source_target_pairs={{0,4},{2,6},{4,8},{6,10},{8,12},{10,14},{12,16},{14,18},{16,20},{1... | collective-permute-start | bytes 442376
  212.5 2.9 %collective-permute-start = (f32[16,2304]{1,0:T(8,128)S(1)}, f32[16,2304]{1,0:T(8,128)S(1)}, u32[]{:S(2)}, u32[]{:S(2)}) collective-permute-start(f32[16,2304]{1,0:T(8,128)S(1)} %fusion), channel_id=1, source_target_pairs={{0,2},{2,4},{4,6},{6,8},{8,10},{10,12},{12,14},{14,16},{16,18},{18... | collective-permute-start | bytes 442376
  215.4 4.1 %collective-permute-start.3 = (f32[12,2304]{1,0:T(8,128)S(1)}, f32[12,2304]{1,0:T(8,128)S(1)}, u32[]{:S(2)}, u32[]{:S(2)}) collective-permute-start(f32[12,2304]{1,0:T(8,128)S(1)} %slice.20), channel_id=1, source_target_pairs={{0,8},{2,10},{4,12},{6,14},{8,16},{10,18},{12,20},{14,22},{16,24},... | collective-permute-start | bytes 331784
  219.5 2.3 fusion.19
  221.8 1.1 fusion.5
  222.9 0.8 concatenate
  223.7 0.7 constant_dynamic-slice_fusion
  224.4 3.3 %reduce_sum.49 = f32[2,16,2304]{2,1,0:T(8,128)} reduce(f32[16,2,16,2304]{3,2,1,0:T(8,128)} %bitcast.67, f32[]{:T(128)} %constant.14.clone.1), dimensions={0}, to_apply=%region_10.0 | reduce | flops 1105920 | bytes 5013508 | tf_op jit(solution)/shard_map/reduce_sum | solution.py:99
  (27 shorter events, 0.6 us)
Async XLA Ops:
  7.2 39.6 %copy-start = (bf16[2,16,2304]{2,1,0:T(8,128)(2,1)S(1)}, bf16[2,16,2304]{2,1,0:T(8,128)(2,1)}, u32[]{:S(2)}) copy-start(bf16[2,16,2304]{2,1,0:T(8,128)(2,1)} %param.8) | copy-start | bytes 442372
  7.2 110.4 %all-reduce.6.cloned.1.call-start = ((), (), s32[]{:S(2)}) async-start(), calls=%async_computation.1 | async-start | bytes 3833856 | tf_op jit(solution)/shard_map/psum | solution.py:54
  34.1 13.7 %copy-start.1 = (bf16[2,2304,2304]{2,1,0:T(8,128)(2,1)S(1)}, bf16[2,2304,2304]{2,1,0:T(8,128)(2,1)}, u32[]{:S(2)}) copy-start(bf16[2,2304,2304]{2,1,0:T(8,128)(2,1)} %param.7) | copy-start | bytes 63700996
  51.3 173.0 %all-gather.4.cloned.1.call-start = ((), (), s32[]{:S(2)}) async-start(), calls=%async_computation | async-start | bytes 5013504 | tf_op jit(solution)/shard_map/all_gather | solution.py:99
  51.9 19.0 %copy-start.4 = (bf16[96,2304]{1,0:T(8,128)(2,1)S(1)}, bf16[96,2304]{1,0:T(8,128)(2,1)}, u32[]{:S(2)}) copy-start(bf16[96,2304]{1,0:T(8,128)(2,1)} %param.11) | copy-start | bytes 1327108
  51.9 65.6 %copy-start.2 = (bf16[2,16,2304]{2,1,0:T(8,128)(2,1)S(1)}, bf16[2,16,2304]{2,1,0:T(8,128)(2,1)}, u32[]{:S(2)}) copy-start(bf16[2,16,2304]{2,1,0:T(8,128)(2,1)} %param.9) | copy-start | bytes 442372
  61.4 57.3 %copy-start.5 = (f32[2,2304]{1,0:T(2,128)S(1)}, f32[2,2304]{1,0:T(2,128)}, u32[]{:S(2)}) copy-start(f32[2,2304]{1,0:T(2,128)} %param.10) | copy-start | bytes 55300
  126.7 20.6 %copy-start.6 = (u32[32]{0:T(128)S(1)}, u32[32]{0:T(128)}, u32[]{:S(2)}) copy-start(u32[32]{0:T(128)} %constant.33) | copy-start | bytes 388
  161.5 60.3 %copy-start.3 = (bf16[2,16,2304]{2,1,0:T(8,128)(2,1)S(1)}, bf16[2,16,2304]{2,1,0:T(8,128)(2,1)}, u32[]{:S(2)}) copy-start(bf16[2,16,2304]{2,1,0:T(8,128)(2,1)} %get-tuple-element.13) | copy-start | bytes 442372
  208.4 14.5 %collective-permute-start.2 = (f32[16,2304]{1,0:T(8,128)S(1)}, f32[16,2304]{1,0:T(8,128)S(1)}, u32[]{:S(2)}, u32[]{:S(2)}) collective-permute-start(f32[16,2304]{1,0:T(8,128)S(1)} %fusion), channel_id=1, source_target_pairs={{0,6},{2,8},{4,10},{6,12},{8,14},{10,16},{12,18},{14,20},{16,22},{... | collective-permute-start | bytes 442376
  209.7 13.2 %collective-permute-start.1 = (f32[16,2304]{1,0:T(8,128)S(1)}, f32[16,2304]{1,0:T(8,128)S(1)}, u32[]{:S(2)}, u32[]{:S(2)}) collective-permute-start(f32[16,2304]{1,0:T(8,128)S(1)} %fusion), channel_id=1, source_target_pairs={{0,4},{2,6},{4,8},{6,10},{8,12},{10,14},{12,16},{14,18},{16,20},{1... | collective-permute-start | bytes 442376
  212.5 10.5 %collective-permute-start = (f32[16,2304]{1,0:T(8,128)S(1)}, f32[16,2304]{1,0:T(8,128)S(1)}, u32[]{:S(2)}, u32[]{:S(2)}) collective-permute-start(f32[16,2304]{1,0:T(8,128)S(1)} %fusion), channel_id=1, source_target_pairs={{0,2},{2,4},{4,6},{6,8},{8,10},{10,12},{12,14},{14,16},{16,18},{18... | collective-permute-start | bytes 442376
  215.4 7.5 %collective-permute-start.3 = (f32[12,2304]{1,0:T(8,128)S(1)}, f32[12,2304]{1,0:T(8,128)S(1)}, u32[]{:S(2)}, u32[]{:S(2)}) collective-permute-start(f32[12,2304]{1,0:T(8,128)S(1)} %slice.20), channel_id=1, source_target_pairs={{0,8},{2,10},{4,12},{6,14},{8,16},{10,18},{12,20},{14,22},{16,24},... | collective-permute-start | bytes 331784
Sparse Core Ops, SparseCore 0:
  51.5 66.0 all-reduce.5
  147.4 68.1 all-gather.3
